TPU v7x, 32 devices: a whole 2x2x4 slice. The times are simulated.
32 devices in a mesh: seg: 8 (over z, y), bins: 4 (over x, core).
Axes of the slice: x: 2, y: 2, z: 4, core: 2. Of those that a mesh axis runs over, the one named last changes fastest.
Arguments:
- segment_maps: float32 [8, 32, 65536], P('seg', None, 'bins'), may hold values from 0 to 8
- bin_shifts: int32 [8, 32], P('seg'), may hold values from -64 to 64, as said below
- window_start: int32 [256], replicated, may hold values from 0 to 7
- window_length: int32 [256], replicated, may hold values from 1 to 8, as said below
Outputs:
- peak_score: float32 [32, 65536], P(None, ('bins', 'seg'))
Inputs may be any that keep to these rules, and one draw needn't show every extreme that they name: `bin_shifts`: both 64 and -64 occur in every draw. window_start + window_length <= 8 for every window; every draw has a window of all 8 segments and a window of one segment.
All inputs are finite; a program needn't handle non-finite values.
Results may differ from a plain program's by a relative error of at most 0.0003.
Values sent between devices are 32-bit elements; how exact they have to be, the bound alone decides.
A program may use at most 256 MiB of HBM per device.

v0:
```python
import jax
import jax.numpy as jnp
from jax import lax
from jax.sharding import PartitionSpec as P

HALO = 64


def padded(cells, sides, width):
    for axis, dim in sides:
        count = lax.axis_size(axis)
        ends = count - 1
        head = lax.slice_in_dim(cells, 0, width, axis=dim)
        tail = lax.slice_in_dim(cells, cells.shape[dim] - width, cells.shape[dim], axis=dim)
        cells = jnp.concatenate(
            [
                lax.ppermute(tail, axis, [(i, (i + 1) % count) for i in range(ends)]),
                cells,
                lax.ppermute(head, axis, [((i + 1) % count, i) for i in range(ends)]),
            ],
            axis=dim,
        )
    return cells


def align_rows(widened, amounts, band):
    values = widened
    sections = (2 * HALO).bit_length()
    for section in range(sections):
        step = 1 << section
        moved = jnp.pad(values[:, :, step:], ((0, 0), (0, 0), (0, step)))
        chosen = (amounts >> section & 1)[:, :, None] == 1
        values = jnp.where(chosen, moved, values)
    return values[:, :, :band]


def on_device(segment_maps, bin_shifts, window_start, window_length):
    widened = padded(segment_maps, (("bins", 2),), HALO)
    band = segment_maps.shape[2]
    aligned = align_rows(widened, bin_shifts + HALO, band)
    received = lax.all_to_all(aligned, "seg", split_axis=2, concat_axis=0, tiled=True)
    cumulative = jnp.cumsum(received, axis=0)
    prefix = jnp.concatenate(
        [jnp.zeros((1,) + cumulative.shape[1:], jnp.float32), cumulative], axis=0
    )
    finish_all = window_start + window_length
    weight_all = window_length.astype(jnp.float32)
    window_group = min(64, window_start.shape[0])
    rounds = window_start.shape[0] // window_group

    def visit_group(position, highest):
        opening = position * window_group
        begins = lax.dynamic_slice_in_dim(window_start, opening, window_group)
        finish = lax.dynamic_slice_in_dim(finish_all, opening, window_group)
        widths = lax.dynamic_slice_in_dim(weight_all, opening, window_group)[:, None, None]
        totals = jnp.take(prefix, finish, axis=0) - jnp.take(prefix, begins, axis=0)
        scores = (totals - 4.0 * widths) / jnp.sqrt(8.0 * widths)
        return jnp.maximum(highest, jnp.max(scores, axis=0))

    initial = jnp.full(prefix.shape[1:], -jnp.inf, jnp.float32)
    return lax.fori_loop(0, rounds, visit_group, initial)


def solution(mesh):
    return jax.shard_map(
        on_device,
        mesh=mesh,
        in_specs=(P("seg", None, "bins"), P("seg", None), P(), P()),
        out_specs=P(None, ("bins", "seg")),
        check_vma=False,
    )
```

profile of v0, /device:TPU:9, one launch (start us, length us, event | category | flops | bytes accessed | tf_op | source)
XLA Modules:
  0.0 413.4 jit_solution(16801159539631823321)
XLA Ops:
  12.6 12.2 %copy.11 = f32[1,32,16512]{1,0,2:T(1,128)} copy(f32[1,32,16512]{2,1,0:T(8,128)S(1)} %concatenate.6) | data formatting | bytes 4227072 | tf_op jit(solution)/shard_map/concatenate | solution.py:15
  30.6 11.1 %broadcast_select_fusion = f32[1,32,16512]{1,0,2:T(1,128)S(1)} fusion(f32[1,32,16512]{1,0,2:T(1,128)S(1)} %copy-done, pred[32]{0:T(512)(128)(4,1)S(1)} %get-tuple-element.185, f32[1,32,16511]{1,0,2:T(1,128)S(1)} %slice-done), kind=kLoop, calls=%fused_computation.15 | loop fusion | flops 528384 | bytes 6340512 | tf_op jit(solution)/shard_map/jit(_where)/select_n | solution.py:33
  43.0 11.2 %broadcast_select_fusion.1 = f32[1,32,16512]{1,0,2:T(1,128)S(1)} fusion(f32[1,32,16512]{1,0,2:T(1,128)S(1)} %broadcast_select_fusion, pred[32]{0:T(512)(128)(4,1)S(1)} %get-tuple-element.184, f32[1,32,16510]{1,0,2:T(1,128)S(1)} %slice.49), kind=kLoop, calls=%fused_computation.16 | loop fusion | flops 528384 | bytes 6340384 | tf_op jit(solution)/shard_map/jit(_where)/select_n | solution.py:33
  55.7 11.2 %broadcast_select_fusion.2 = f32[1,32,16512]{1,0,2:T(1,128)S(1)} fusion(f32[1,32,16512]{1,0,2:T(1,128)S(1)} %broadcast_select_fusion.1, pred[32]{0:T(512)(128)(4,1)S(1)} %get-tuple-element.183, f32[1,32,16508]{1,0,2:T(1,128)S(1)} %slice.50), kind=kLoop, calls=%fused_computation.17 | loop fusion | flops 528384 | bytes 6340128 | tf_op jit(solution)/shard_map/jit(_where)/select_n | solution.py:33
  67.8 11.2 %broadcast_select_fusion.3 = f32[1,32,16512]{1,0,2:T(1,128)S(1)} fusion(f32[1,32,16512]{1,0,2:T(1,128)S(1)} %broadcast_select_fusion.2, pred[32]{0:T(512)(128)(4,1)S(1)} %get-tuple-element.182, f32[1,32,16504]{1,0,2:T(1,128)S(1)} %slice.51), kind=kLoop, calls=%fused_computation.18 | loop fusion | flops 528384 | bytes 6339616 | tf_op jit(solution)/shard_map/jit(_where)/select_n | solution.py:33
  80.2 11.4 %broadcast_select_fusion.4 = f32[1,32,16512]{1,0,2:T(1,128)S(1)} fusion(f32[1,32,16512]{1,0,2:T(1,128)S(1)} %broadcast_select_fusion.3, pred[32]{0:T(512)(128)(4,1)S(1)} %get-tuple-element.181, f32[1,32,16496]{1,0,2:T(1,128)S(1)} %slice.52), kind=kLoop, calls=%fused_computation.19 | loop fusion | flops 528384 | bytes 6338592 | tf_op jit(solution)/shard_map/jit(_where)/select_n | solution.py:33
  92.7 11.6 %broadcast_select_fusion.5 = f32[1,32,16512]{1,0,2:T(1,128)S(1)} fusion(f32[1,32,16512]{1,0,2:T(1,128)S(1)} %broadcast_select_fusion.4, pred[32]{0:T(512)(128)(4,1)S(1)} %get-tuple-element.180, f32[1,32,16480]{1,0,2:T(1,128)S(1)} %slice.53), kind=kLoop, calls=%fused_computation.20 | loop fusion | flops 528384 | bytes 6336544 | tf_op jit(solution)/shard_map/jit(_where)/select_n | solution.py:33
  105.4 12.1 %broadcast_select_fusion.6 = f32[1,32,16512]{1,0,2:T(1,128)S(1)} fusion(f32[1,32,16512]{1,0,2:T(1,128)S(1)} %broadcast_select_fusion.5, pred[32]{0:T(512)(128)(4,1)S(1)} %get-tuple-element.179, f32[1,32,16448]{1,0,2:T(1,128)S(1)} %slice.54), kind=kLoop, calls=%fused_computation.21 | loop fusion | flops 528384 | bytes 6332448 | tf_op jit(solution)/shard_map/jit(_where)/select_n | solution.py:33
  118.4 11.6 %fusion.5 = f32[16384,1,32]{2,1,0:T(1,128)} fusion(f32[1,32,16512]{1,0,2:T(1,128)S(1)} %broadcast_select_fusion.6, f32[1,32,16384]{1,0,2:T(1,128)S(1)} %slice.55, pred[32]{0:T(512)(128)(4,1)S(1)} %get-tuple-element.186), kind=kLoop, calls=%fused_computation.34 | loop fusion | flops 524288 | bytes 6291488
  130.6 74.4 %reduce = f32[16384,32]{1,0:T(8,128)} reduce(f32[16384,1,32]{2,1,0:T(1,128)} %fusion.5, f32[]{:T(128)} %broadcast.127), dimensions={1}, to_apply=%fusion.5.reduce_sub_computation | reduce | bytes 4194308
  205.0 8.6 %reshape.120 = f32[8,1,65536]{2,1,0:T(1,128)} reshape(f32[16384,32]{1,0:T(8,128)} %reduce) | data formatting | bytes 4194304
  219.3 45.4 %all-to-all-done = f32[8,1,65536]{2,1,0:T(1,128)} async-done(((f32[8,1,65536]{2,1,0:T(1,128)}), f32[8,1,65536]{2,1,0:T(1,128)}, u32[]{:S(2)}, u32[]{:S(2)}) %all-to-all-start) | async-done | bytes 2097184 | tf_op jit(solution)/shard_map/all_to_all | solution.py:41
  271.9 17.6 %reshape.121 = f32[16384,1,32]{2,1,0:T(1,128)} reshape(f32[8,65536]{1,0:T(8,128)S(1)} %reduce.1) | data formatting | bytes 4194304
  304.2 108.4 %while.14 = (s32[]{:T(128)}, f32[32,2048]{1,0:T(8,128)S(1)}, s32[256]{0:T(256)S(1)}, f32[9,32,2048]{2,1,0:T(8,128)S(1)}, s32[256]{0:T(256)S(1)}, /*index=5*/f32[...) while((s32[]{:T(128)}, f32[32,2048]{1,0:T(8,128)S(1)}, s32[256]{0:T(256)S(1)}, ...), condition=%wide.region_3.5_spmd.clone, body=%wide.region_1.4_spmd.clone.sunk | while | flops 25234308 | bytes 101723808 | solution.py:61
  304.3 7.3 %gather_fusion = f32[64,32,2048]{2,1,0:T(8,128)} fusion(f32[9,32,2048]{2,1,0:T(8,128)S(1)} %get-tuple-element.259, s32[1024]{0:T(1024)S(1)} %pad_clamp_fusion.4), kind=kCustom, calls=%fused_computation.1.clone.clone.1 | custom fusion | bytes 33554688 | tf_op jit(solution)/shard_map/while/body/eval_jaxpr/jit(_take)/gather | solution.py:56
  311.7 7.3 %gather_fusion.1 = f32[64,32,2048]{2,1,0:T(8,128)} fusion(f32[9,32,2048]{2,1,0:T(8,128)S(1)} %get-tuple-element.259, s32[1024]{0:T(1024)S(1)} %pad_clamp_fusion.5), kind=kCustom, calls=%fused_computation.clone.clone.1 | custom fusion | bytes 33554688 | tf_op jit(solution)/shard_map/while/body/eval_jaxpr/jit(_take)/gather | solution.py:56
  319.1 12.1 %fusion.7 = f32[32,2048]{1,0:T(8,128)S(1)} fusion(f32[64,32,2048]{2,1,0:T(8,128)} %gather_fusion, f32[64,32,2048]{2,1,0:T(8,128)} %gather_fusion.1, f32[64]{0:T(128)S(1)} %get-tuple-element.232, f32[64]{0:T(128)S(1)} %get-tuple-element.233, pred[64]{0:T(512)(128)(4,1)S(1)} %get-tuple-element.234, pred[64]{0:T(512)(128)(4,1)S(1)} %get-tuple-element.235), kind=kLoop, calls=%fused_computation.5.clone.1 | loop fusion | flops 25100288 | bytes 33817216 | tf_op jit(solution)/shard_map/while/body/eval_jaxpr/reduce_max | solution.py:58
  331.4 7.3 %gather_fusion = f32[64,32,2048]{2,1,0:T(8,128)} fusion(f32[9,32,2048]{2,1,0:T(8,128)S(1)} %get-tuple-element.259, s32[1024]{0:T(1024)S(1)} %pad_clamp_fusion.4), kind=kCustom, calls=%fused_computation.1.clone.clone.1 | custom fusion | bytes 33554688 | tf_op jit(solution)/shard_map/while/body/eval_jaxpr/jit(_take)/gather | solution.py:56
  338.8 7.3 %gather_fusion.1 = f32[64,32,2048]{2,1,0:T(8,128)} fusion(f32[9,32,2048]{2,1,0:T(8,128)S(1)} %get-tuple-element.259, s32[1024]{0:T(1024)S(1)} %pad_clamp_fusion.5), kind=kCustom, calls=%fused_computation.clone.clone.1 | custom fusion | bytes 33554688 | tf_op jit(solution)/shard_map/while/body/eval_jaxpr/jit(_take)/gather | solution.py:56
  346.2 12.1 %fusion.7 = f32[32,2048]{1,0:T(8,128)S(1)} fusion(f32[64,32,2048]{2,1,0:T(8,128)} %gather_fusion, f32[64,32,2048]{2,1,0:T(8,128)} %gather_fusion.1, f32[64]{0:T(128)S(1)} %get-tuple-element.232, f32[64]{0:T(128)S(1)} %get-tuple-element.233, pred[64]{0:T(512)(128)(4,1)S(1)} %get-tuple-element.234, pred[64]{0:T(512)(128)(4,1)S(1)} %get-tuple-element.235), kind=kLoop, calls=%fused_computation.5.clone.1 | loop fusion | flops 25100288 | bytes 33817216 | tf_op jit(solution)/shard_map/while/body/eval_jaxpr/reduce_max | solution.py:58
  358.5 7.3 %gather_fusion = f32[64,32,2048]{2,1,0:T(8,128)} fusion(f32[9,32,2048]{2,1,0:T(8,128)S(1)} %get-tuple-element.259, s32[1024]{0:T(1024)S(1)} %pad_clamp_fusion.4), kind=kCustom, calls=%fused_computation.1.clone.clone.1 | custom fusion | bytes 33554688 | tf_op jit(solution)/shard_map/while/body/eval_jaxpr/jit(_take)/gather | solution.py:56
  373.3 12.1 %fusion.7 = f32[32,2048]{1,0:T(8,128)S(1)} fusion(f32[64,32,2048]{2,1,0:T(8,128)} %gather_fusion, f32[64,32,2048]{2,1,0:T(8,128)} %gather_fusion.1, f32[64]{0:T(128)S(1)} %get-tuple-element.232, f32[64]{0:T(128)S(1)} %get-tuple-element.233, pred[64]{0:T(512)(128)(4,1)S(1)} %get-tuple-element.234, pred[64]{0:T(512)(128)(4,1)S(1)} %get-tuple-element.235), kind=kLoop, calls=%fused_computation.5.clone.1 | loop fusion | flops 25100288 | bytes 33817216 | tf_op jit(solution)/shard_map/while/body/eval_jaxpr/reduce_max | solution.py:58
  385.7 7.3 %gather_fusion = f32[64,32,2048]{2,1,0:T(8,128)} fusion(f32[9,32,2048]{2,1,0:T(8,128)S(1)} %get-tuple-element.259, s32[1024]{0:T(1024)S(1)} %pad_clamp_fusion.4), kind=kCustom, calls=%fused_computation.1.clone.clone.1 | custom fusion | bytes 33554688 | tf_op jit(solution)/shard_map/while/body/eval_jaxpr/jit(_take)/gather | solution.py:56
  400.4 12.1 %fusion.7 = f32[32,2048]{1,0:T(8,128)S(1)} fusion(f32[64,32,2048]{2,1,0:T(8,128)} %gather_fusion, f32[64,32,2048]{2,1,0:T(8,128)} %gather_fusion.1, f32[64]{0:T(128)S(1)} %get-tuple-element.232, f32[64]{0:T(128)S(1)} %get-tuple-element.233, pred[64]{0:T(512)(128)(4,1)S(1)} %get-tuple-element.234, pred[64]{0:T(512)(128)(4,1)S(1)} %get-tuple-element.235), kind=kLoop, calls=%fused_computation.5.clone.1 | loop fusion | flops 25100288 | bytes 33817216 | tf_op jit(solution)/shard_map/while/body/eval_jaxpr/reduce_max | solution.py:58
  (55 shorter events, 70.7 us)
Async XLA Ops:
  0.8 6.3 %collective-permute-start = (f32[1,32,64]{2,1,0:T(8,128)S(1)}, f32[1,32,64]{2,1,0:T(8,128)S(1)}, u32[]{:S(2)}, u32[]{:S(2)}) collective-permute-start(f32[1,32,64]{2,1,0:T(8,128)S(1)} %get-tuple-element.176), channel_id=1, source_target_pairs={{0,1},{1,2},{2,3},{4,5},{5,6},{6,7},{8,9},{9,10},{10,11},{12,13},{... | collective-permute-start | bytes 24584 | tf_op jit(solution)/shard_map/ppermute | solution.py:17
  4.5 5.1 %collective-permute-start.1 = (f32[1,32,64]{2,1,0:T(8,128)S(1)}, f32[1,32,64]{2,1,0:T(8,128)S(1)}, u32[]{:S(2)}, u32[]{:S(2)}) collective-permute-start(f32[1,32,64]{2,1,0:T(8,128)S(1)} %get-tuple-element.175), channel_id=1, source_target_pairs={{1,0},{2,1},{3,2},{5,4},{6,5},{7,6},{9,8},{10,9},{11,10},{13,12},{... | collective-permute-start | bytes 24584 | tf_op jit(solution)/shard_map/ppermute | solution.py:19
  24.8 3.4 copy-start
  24.8 5.8 %slice-start = ((f32[1,32,16512]{1,0,2:T(1,128)}), f32[1,32,16511]{1,0,2:T(1,128)S(1)}, s32[]{:S(2)}) async-start(f32[1,32,16512]{1,0,2:T(1,128)} %copy.11), calls=%async_computation.1 | async-start | bytes 16907264 | tf_op jit(solution)/shard_map/slice | solution.py:31
  205.0 14.3 %copy-start.2 = (s32[256]{0:T(256)S(1)}, s32[256]{0:T(256)}, u32[]{:S(2)}) copy-start(s32[256]{0:T(256)} %param.10) | copy-start | bytes 3076
  205.0 14.3 %copy-start.3 = (s32[256]{0:T(256)S(1)}, s32[256]{0:T(256)}, u32[]{:S(2)}) copy-start(s32[256]{0:T(256)} %param.11) | copy-start | bytes 3076
  213.6 51.1 %all-to-all-start = ((f32[8,1,65536]{2,1,0:T(1,128)}), f32[8,1,65536]{2,1,0:T(1,128)}, u32[]{:S(2)}, u32[]{:S(2)}) async-start(f32[8,1,65536]{2,1,0:T(1,128)} %reshape.120), calls=%async_computation | async-start | bytes 4194304 | tf_op jit(solution)/shard_map/all_to_all | solution.py:41
  412.7 0.7 copy-start.1
where the time goes:
time: 417 us; the launch traced here: 413 us
  other arithmetic  229 us (55%)
  local copies, waits for them, and re-layouts  124 us (30%)
  waiting for transfers between devices  47.8 us (11%)
  starting transfers between devices  11.3 us (3%)
    unnamed x3, other arithmetic  86.1 us
    select_n x7, other arithmetic, align_rows(): values = jnp.where(chosen, moved, values)  79.8 us
    gather x8, local copies, waits for them, and re-layouts, visit_group(): totals = jnp.take(prefix, finish, axis=0) - jnp.take(prefix, begins, axis=0)  58.7 us
    reduce_max x4, other arithmetic, visit_group(): return jnp.maximum(highest, jnp.max(scores, axis=0))  48.5 us
    all_to_all x1, waiting for transfers between devices, on_device(): lax.all_to_all(aligned, 'seg', split_axis=2, concat_axis=0, tiled=True)  45.4 us
    unnamed x12, local copies, waits for them, and re-layouts  33.7 us
    concatenate x2, local copies, waits for them, and re-layouts, padded(): jnp.concatenate([lax.ppermute(tail, axis, [(i, (i + 1) % count) for i in...  15.2 us
    slice x9, local copies, waits for them, and re-layouts, align_rows(): moved = jnp.pad(values[:, :, step:], ((0, 0), (0, 0), (0, step)))  10.3 us
  transfers between devices with their start and end apart: 3, of which 2 were waited for; matrix products, arithmetic and copies ran while one was open for 0% of the time, Pallas kernels for 0%

commit v1 on v0

v1 whole, which is shorter than its diff:
```python
import functools
import math

import jax
import jax.numpy as jnp
from jax import lax
from jax.experimental import pallas as pl
from jax.experimental.pallas import tpu as pltpu
from jax.sharding import PartitionSpec as P

MESH = pl.DeviceIdType.MESH
LANES = 128
ROWS = 8


def nearest(me, rank, n):
    short = jnp.minimum(me, n - 1 - me)
    up = me < n - 1 - me
    half = (rank + 1) // 2
    both = jnp.where(rank % 2 == 1, half, -half)
    rest = jnp.where(up, rank - short, short - rank)
    return me + jnp.where(rank <= 2 * short, both, rest)


def kernel(n, bands, by_pairs, maps, shifts, starts, lengths, out, wide, blocks, shift_rows, table,
           in_sem, send_sem, recv_sem, halo_send, halo_recv):
    me, band = lax.axis_index("seg"), lax.axis_index("bins")
    spins, bins = maps.shape[1], maps.shape[2]
    width = out.shape[1]
    tiles = width // LANES
    chunks = spins // ROWS
    windows = starts.shape[0]

    def rows_of(chunk):
        return pl.ds(pl.multiple_of(chunk * ROWS, ROWS), ROWS)

    def loading(chunk):
        return pltpu.make_async_copy(
            maps.at[0, rows_of(chunk), :], wide.at[rows_of(chunk), pl.ds(LANES, bins)], in_sem.at[chunk]
        )

    for chunk in range(chunks):
        loading(chunk).start()

    barrier = pltpu.get_barrier_semaphore()

    def greet(offset, carry):
        peer = lax.rem(me + offset, n)
        pl.semaphore_signal(barrier, inc=1, device_id={"seg": peer}, device_id_type=MESH)
        return carry

    lax.fori_loop(1, n, greet, 0)

    @pl.when(band > 0)
    def _():
        pl.semaphore_signal(barrier, inc=1, device_id={"bins": band - 1}, device_id_type=MESH)

    @pl.when(band < bands - 1)
    def _():
        pl.semaphore_signal(barrier, inc=1, device_id={"bins": band + 1}, device_id_type=MESH)

    @pl.when(band == 0)
    def _():
        wide[:, :LANES] = jnp.zeros((spins, LANES), jnp.float32)

    @pl.when(band == bands - 1)
    def _():
        wide[:, bins + LANES:] = jnp.zeros((spins, LANES), jnp.float32)

    sublane = lax.broadcasted_iota(jnp.int32, (ROWS, LANES), 0)
    lane = lax.broadcasted_iota(jnp.int32, (ROWS, LANES), 1)
    for chunk in range(chunks):
        amounts = jnp.zeros((ROWS, LANES), jnp.int32)
        for row in range(ROWS):
            amounts = jnp.where(sublane == row, shifts[0, chunk * ROWS + row], amounts)
        shift_rows[chunk * ROWS:(chunk + 1) * ROWS, :] = amounts

    neighbours = jnp.where(band > 0, 1, 0) + jnp.where(band < bands - 1, 1, 0)
    pl.semaphore_wait(barrier, n - 1 + neighbours)

    def halo(side, peer):
        source = bins - LANES if side == 0 else 0
        target = 0 if side == 0 else bins + LANES
        return pltpu.make_async_remote_copy(
            src_ref=maps.at[0, :, pl.ds(source, LANES)],
            dst_ref=wide.at[:, pl.ds(target, LANES)],
            send_sem=halo_send.at[side],
            recv_sem=halo_recv.at[side],
            device_id={"bins": peer},
            device_id_type=MESH,
        )

    @pl.when(band < bands - 1)
    def _():
        halo(0, band + 1).start()

    @pl.when(band > 0)
    def _():
        halo(1, band - 1).start()

    def sending(chunk, peer):
        return pltpu.make_async_remote_copy(
            src_ref=blocks.at[0, peer, rows_of(chunk), :],
            dst_ref=blocks.at[1, me, rows_of(chunk), :],
            send_sem=send_sem.at[chunk, peer],
            recv_sem=recv_sem.at[chunk, me],
            device_id={"seg": peer},
            device_id_type=MESH,
        )

    def receiving(chunk, source):
        return pltpu.make_async_remote_copy(
            src_ref=blocks.at[0, source, rows_of(chunk), :],
            dst_ref=blocks.at[1, source, rows_of(chunk), :],
            send_sem=send_sem.at[chunk, source],
            recv_sem=recv_sem.at[chunk, source],
            device_id={"seg": source},
            device_id_type=MESH,
        )

    def step(i, carry):
        chunk, place = i // n, i % n
        own = place == n - 1
        dest = jnp.where(own, me, nearest(me, place + 1, n))

        @pl.when(place == 0)
        def _():
            loading(chunk).wait()

        @pl.when((chunk == 0) & (dest == 0) & (band > 0))
        def _():
            halo(0, band - 1).wait_recv()

        @pl.when((chunk == 0) & (dest == n - 1) & (band < bands - 1))
        def _():
            halo(1, band + 1).wait_recv()

        rows = rows_of(chunk)
        position = lane + shift_rows[rows, :]
        index = position & (LANES - 1)
        below, above = position < 0, position >= LANES

        def turned(tile):
            columns = pl.ds(pl.multiple_of(dest * width + tile * LANES, LANES), LANES)
            return jnp.take_along_axis(wide[rows, columns], index, axis=1, mode="promise_in_bounds")

        side = jnp.where(own, 1, 0)
        before, here = turned(0), turned(1)
        for tile in range(tiles):
            after = turned(tile + 2)
            blocks[side, dest, rows, tile * LANES:(tile + 1) * LANES] = jnp.where(
                below, before, jnp.where(above, after, here)
            )
            before, here = here, after

        @pl.when(place > 0)
        def _():
            sending(chunk, nearest(me, place, n)).start()

        return carry

    lax.fori_loop(0, chunks * n, step, 0)

    lowest = -jnp.inf
    if by_pairs:
        pair = lax.broadcasted_iota(jnp.int32, (n * n, LANES), 0)

        def mark(w, held):
            return jnp.where(pair == starts[w] * n + lengths[w] - 1, 0.0, held)

        table[...] = lax.fori_loop(0, windows, mark, jnp.full((n * n, LANES), lowest, jnp.float32))

    group = 2 * LANES if width % (2 * LANES) == 0 else LANES

    def arrive(chunk):
        def one(source, carry):
            @pl.when(source != me)
            def _():
                receiving(chunk, source).wait_recv()
            return carry
        lax.fori_loop(0, n, one, 0)

    def search_pairs(chunk):
        rows = rows_of(chunk)

        def search(j, carry):
            columns = pl.ds(pl.multiple_of(j * group, group), group)
            prefix = [None]
            for source in range(n):
                value = blocks[1, source, rows, columns]
                prefix.append(value if source == 0 else prefix[-1] + value)
            best = None
            for length in range(1, n + 1):
                most = None
                for start in range(n + 1 - length):
                    total = prefix[length] if start == 0 else prefix[start + length] - prefix[start]
                    at = start * n + length - 1
                    mask = jnp.concatenate([table[at:at + 1, :]] * (group // LANES), axis=1)
                    total = total + mask
                    most = total if most is None else jnp.maximum(most, total)
                root = math.sqrt(8.0 * length)
                score = most * (1.0 / root) - 4.0 * length / root
                best = score if best is None else jnp.maximum(best, score)
            out[rows, columns] = best
            return carry

        lax.fori_loop(0, width // group, search, 0)

    def search_windows(chunk):
        rows = rows_of(chunk)
        table[0] = jnp.zeros((ROWS, width), jnp.float32)

        def add(source, total):
            total = total + blocks[1, source, rows, :]
            table[source + 1] = total
            return total

        lax.fori_loop(0, n, add, jnp.zeros((ROWS, width), jnp.float32))

        def search(w, best):
            total = table[starts[w] + lengths[w]] - table[starts[w]]
            weight = jnp.full((ROWS, width), lengths[w], jnp.int32).astype(jnp.float32)
            return jnp.maximum(best, (total - 4.0 * weight) / jnp.sqrt(8.0 * weight))

        out[rows, :] = lax.fori_loop(0, windows, search, jnp.full((ROWS, width), lowest, jnp.float32))

    def finish(chunk, carry):
        arrive(chunk)
        (search_pairs if by_pairs else search_windows)(chunk)
        return carry

    lax.fori_loop(0, chunks, finish, 0)

    def drain(i, carry):
        chunk, peer = i // n, i % n

        @pl.when(peer != me)
        def _():
            sending(chunk, peer).wait_send()
        return carry

    lax.fori_loop(0, chunks * n, drain, 0)

    @pl.when(band < bands - 1)
    def _():
        halo(0, band + 1).wait_send()

    @pl.when(band > 0)
    def _():
        halo(1, band - 1).wait_send()


def solution(mesh):
    n, bands = mesh.shape["seg"], mesh.shape["bins"]

    def on_device(segment_maps, bin_shifts, window_start, window_length):
        _, spins, bins = segment_maps.shape
        width = bins // n
        chunks = spins // ROWS
        by_pairs = n * (n + 1) // 2 <= window_start.shape[0]
        table = (n * n, LANES) if by_pairs else (n + 1, ROWS, width)
        smem = pl.BlockSpec(memory_space=pltpu.SMEM)
        return pl.pallas_call(
            functools.partial(kernel, n, bands, by_pairs),
            out_shape=jax.ShapeDtypeStruct((spins, width), jnp.float32),
            in_specs=[pl.BlockSpec(memory_space=pl.ANY), smem, smem, smem],
            out_specs=pl.BlockSpec(memory_space=pltpu.VMEM),
            scratch_shapes=[
                pltpu.VMEM((spins, bins + 2 * LANES), jnp.float32),
                pltpu.VMEM((2, n, spins, width), jnp.float32),
                pltpu.VMEM((spins, LANES), jnp.int32),
                pltpu.VMEM(table, jnp.float32),
                pltpu.SemaphoreType.DMA((chunks,)),
                pltpu.SemaphoreType.DMA((chunks, n)),
                pltpu.SemaphoreType.DMA((chunks, n)),
                pltpu.SemaphoreType.DMA((2,)),
                pltpu.SemaphoreType.DMA((2,)),
            ],
            compiler_params=pltpu.CompilerParams(collective_id=0, has_side_effects=True),
        )(segment_maps, bin_shifts, window_start, window_length)

    return jax.shard_map(
        on_device,
        mesh=mesh,
        in_specs=(P("seg", None, "bins"), P("seg", None), P(), P()),
        out_specs=P(None, ("bins", "seg")),
        check_vma=False,
    )
```

time: 417 us -> 58.5 us (0.14)
  the two profiles are of different devices: /device:TPU:9 before, /device:TPU:1 now
where the time goes in v1:
time: 58.5 us; the launch traced here: 58.3 us
  Pallas kernels  56.7 us (97%)
  local copies, waits for them, and re-layouts  1.67 us (3%)
    pallas_call x1, Pallas kernels, on_device(): pl.pallas_call(functools.partial(kernel, n, bands, by_pairs), out_shape=j...  56.7 us
    unnamed x1, local copies, waits for them, and re-layouts  1.67 us

profile of v1, /device:TPU:1, one launch (start us, length us, event | category | flops | bytes accessed | tf_op | source)
XLA Modules:
  0.0 58.3 jit_solution(13204243792039905476)
XLA Ops:
  0.0 56.7 %shard_map.46 = f32[32,2048]{1,0:T(8,128)} custom-call(f32[1,32,16384]{2,1,0:T(8,128)} %maps.1, s32[1,32]{1,0:T(1,128)} %shifts.1, s32[256]{0:T(256)} %starts.1, s32[256]{0:T(256)} %lengths.1), custom_call_target="tpu_custom_call" | custom-call | tf_op jit(solution)/shard_map/pallas_call | solution.py:263
  56.7 1.7 %copy.6 = f32[32,2048]{1,0:T(8,128)} copy(f32[32,2048]{1,0:T(8,128)} %shard_map.46) | data formatting | bytes 524288

commit v2 on v1

--- a/solution.py
+++ b/solution.py
@@ -13,13 +13,18 @@
 ROWS = 8
 
 
-def nearest(me, rank, n):
-    short = jnp.minimum(me, n - 1 - me)
-    up = me < n - 1 - me
-    half = (rank + 1) // 2
-    both = jnp.where(rank % 2 == 1, half, -half)
-    rest = jnp.where(up, rank - short, short - rank)
-    return me + jnp.where(rank <= 2 * short, both, rest)
+def order(me, place, n):
+    stride = n // 2
+    first, partner = 0, place + stride
+    while stride > 1:
+        first += stride
+        stride //= 2
+        partner = jnp.where(place >= first, place - first + stride, partner)
+    other, bit = 0, 1
+    while bit < n:
+        other = other + (me // bit + partner // bit) % 2 * bit
+        bit *= 2
+    return other
 
 
 def kernel(n, bands, by_pairs, maps, shifts, starts, lengths, out, wide, blocks, shift_rows, table,
@@ -121,7 +126,7 @@
     def step(i, carry):
         chunk, place = i // n, i % n
         own = place == n - 1
-        dest = jnp.where(own, me, nearest(me, place + 1, n))
+        dest = jnp.where(own, me, order(me, place, n))
 
         @pl.when(place == 0)
         def _():
@@ -155,7 +160,7 @@
 
         @pl.when(place > 0)
         def _():
-            sending(chunk, nearest(me, place, n)).start()
+            sending(chunk, order(me, place - 1, n)).start()
 
         return carry
 
@@ -262,7 +267,7 @@
         smem = pl.BlockSpec(memory_space=pltpu.SMEM)
         return pl.pallas_call(
             functools.partial(kernel, n, bands, by_pairs),
-            out_shape=jax.ShapeDtypeStruct((spins, width), jnp.float32),
+            out_shape=pltpu.VMEM((spins, width), jnp.float32),
             in_specs=[pl.BlockSpec(memory_space=pl.ANY), smem, smem, smem],
             out_specs=pl.BlockSpec(memory_space=pltpu.VMEM),
             scratch_shapes=[

time: 58.5 us -> 54 us (0.923)
  the two profiles are of different devices: /device:TPU:1 before, /device:TPU:9 now
where the time goes in v2:
time: 54 us; the launch traced here: 53.9 us
  Pallas kernels  53.2 us (99%)
  local copies, waits for them, and re-layouts  0.71 us (1%)
    pallas_call x1, Pallas kernels, on_device(): pl.pallas_call(functools.partial(kernel, n, bands, by_pairs), out_shape=p...  53.2 us

profile of v2, /device:TPU:9, one launch (start us, length us, event | category | flops | bytes accessed | tf_op | source)
XLA Modules:
  0.0 53.9 jit_solution(5151464335230624249)
XLA Ops:
  0.0 53.2 %shard_map.46 = f32[32,2048]{1,0:T(8,128)S(1)} custom-call(f32[1,32,16384]{2,1,0:T(8,128)} %maps.1, s32[1,32]{1,0:T(1,128)} %shifts.1, s32[256]{0:T(256)} %starts.1, s32[256]{0:T(256)} %lengths.1), custom_call_target="tpu_custom_call" | custom-call | tf_op jit(solution)/shard_map/pallas_call | solution.py:268
  53.2 0.7 %copy.6 = f32[32,2048]{1,0:T(8,128)} copy(f32[32,2048]{1,0:T(8,128)S(1)} %shard_map.46) | data formatting | bytes 524288

commit v3 on v2

--- a/solution.py
+++ b/solution.py
@@ -20,15 +20,23 @@
         first += stride
         stride //= 2
         partner = jnp.where(place >= first, place - first + stride, partner)
+    return flipped(me, partner, n)
+
+
+def flipped(me, mask, n):
     other, bit = 0, 1
     while bit < n:
-        other = other + (me // bit + partner // bit) % 2 * bit
+        other = other + (me // bit + mask // bit) % 2 * bit
         bit *= 2
     return other
 
 
-def kernel(n, bands, by_pairs, maps, shifts, starts, lengths, out, wide, blocks, shift_rows, table,
-           in_sem, send_sem, recv_sem, halo_send, halo_recv):
+def twin(me):
+    return me + 1 - 2 * (me % 2)
+
+
+def kernel(n, bands, by_pairs, maps, shifts_in, starts_in, lengths_in, out, wide, blocks, shift_rows, table,
+           shifts, starts, lengths, side_in, all_in, small_sem, in_sem, send_sem, recv_sem, halo_send, halo_recv):
     me, band = lax.axis_index("seg"), lax.axis_index("bins")
     spins, bins = maps.shape[1], maps.shape[2]
     width = out.shape[1]
@@ -44,26 +52,47 @@
             maps.at[0, rows_of(chunk), :], wide.at[rows_of(chunk), pl.ds(LANES, bins)], in_sem.at[chunk]
         )
 
+    barrier = pltpu.get_barrier_semaphore()
+
+    def greet(peer):
+        pl.semaphore_signal(barrier, inc=1, device_id={"seg": peer}, device_id_type=MESH)
+
+    early = n // 2 == 4
+    pairs, pair_at = n // 2, me // 2
+    low = pair_at < pairs // 2
+    inner, outer = jnp.where(low, me + 2, me - 2), jnp.where(low, me - 2, me + 2)
+    middle = jnp.where(low, pair_at == pairs // 2 - 1, pair_at == pairs // 2)
+    has_outer = jnp.where(low, pair_at > 0, pair_at < pairs - 1)
+
+    greet(twin(me))
+
+    @pl.when(middle)
+    def _():
+        greet(inner)
+        greet(twin(inner))
+
+    @pl.when(has_outer)
+    def _():
+        greet(outer)
+        greet(twin(outer))
+
+    @pl.when(band > 0)
+    def _():
+        pl.semaphore_signal(barrier, inc=1, device_id={"bins": band - 1}, device_id_type=MESH)
+
+    @pl.when(band < bands - 1)
+    def _():
+        pl.semaphore_signal(barrier, inc=1, device_id={"bins": band + 1}, device_id_type=MESH)
+
+    small = [
+        pltpu.make_async_copy(here, there, small_sem.at[i])
+        for i, (here, there) in enumerate(((shifts_in, shifts), (starts_in, starts), (lengths_in, lengths)))
+    ]
+    for copy in small:
+        copy.start()
     for chunk in range(chunks):
         loading(chunk).start()
 
-    barrier = pltpu.get_barrier_semaphore()
-
-    def greet(offset, carry):
-        peer = lax.rem(me + offset, n)
-        pl.semaphore_signal(barrier, inc=1, device_id={"seg": peer}, device_id_type=MESH)
-        return carry
-
-    lax.fori_loop(1, n, greet, 0)
-
-    @pl.when(band > 0)
-    def _():
-        pl.semaphore_signal(barrier, inc=1, device_id={"bins": band - 1}, device_id_type=MESH)
-
-    @pl.when(band < bands - 1)
-    def _():
-        pl.semaphore_signal(barrier, inc=1, device_id={"bins": band + 1}, device_id_type=MESH)
-
     @pl.when(band == 0)
     def _():
         wide[:, :LANES] = jnp.zeros((spins, LANES), jnp.float32)
@@ -71,6 +100,9 @@
     @pl.when(band == bands - 1)
     def _():
         wide[:, bins + LANES:] = jnp.zeros((spins, LANES), jnp.float32)
+
+    for copy in small:
+        copy.wait()
 
     sublane = lax.broadcasted_iota(jnp.int32, (ROWS, LANES), 0)
     lane = lax.broadcasted_iota(jnp.int32, (ROWS, LANES), 1)
@@ -81,7 +113,38 @@
         shift_rows[chunk * ROWS:(chunk + 1) * ROWS, :] = amounts
 
     neighbours = jnp.where(band > 0, 1, 0) + jnp.where(band < bands - 1, 1, 0)
-    pl.semaphore_wait(barrier, n - 1 + neighbours)
+    pl.semaphore_wait(barrier, 3 + neighbours)
+
+    def tell(sem, peer):
+        pl.semaphore_signal(sem, inc=1, device_id={"seg": peer}, device_id_type=MESH)
+
+    @pl.when(jnp.logical_not(has_outer))
+    def _():
+        tell(side_in, inner)
+
+    def hear_side():
+        @pl.when(has_outer)
+        def _():
+            pl.semaphore_wait(side_in, 1)
+
+        @pl.when(has_outer & middle)
+        def _():
+            tell(all_in, inner)
+
+        @pl.when(has_outer & jnp.logical_not(middle))
+        def _():
+            tell(side_in, inner)
+
+    def hear_all():
+        pl.semaphore_wait(all_in, 1)
+
+        @pl.when(has_outer)
+        def _():
+            tell(all_in, outer)
+
+    if not early:
+        hear_side()
+        hear_all()
 
     def halo(side, peer):
         source = bins - LANES if side == 0 else 0
@@ -123,10 +186,19 @@
             device_id_type=MESH,
         )
 
+    def partner(chunk, place):
+        later = order(me, place, n)
+        if not early:
+            return later
+        ends, mids = jnp.int32(0), jnp.int32(0)
+        for i, (end, mid) in enumerate(zip((2, 3, 1, 4, 5, 6, 7), (6, 7, 1, 2, 3, 4, 5))):
+            ends, mids = jnp.where(place == i, end, ends), jnp.where(place == i, mid, mids)
+        return jnp.where(chunk == 0, flipped(me, jnp.where(middle, mids, ends), n), later)
+
     def step(i, carry):
         chunk, place = i // n, i % n
         own = place == n - 1
-        dest = jnp.where(own, me, order(me, place, n))
+        dest = jnp.where(own, me, partner(chunk, place))
 
         @pl.when(place == 0)
         def _():
@@ -158,9 +230,18 @@
             )
             before, here = here, after
 
+        if early:
+            @pl.when((chunk == 0) & (place == 4))
+            def _():
+                hear_side()
+
+            @pl.when((chunk == 0) & (place == jnp.where(middle, 6, 4)))
+            def _():
+                hear_all()
+
         @pl.when(place > 0)
         def _():
-            sending(chunk, order(me, place - 1, n)).start()
+            sending(chunk, partner(chunk, place - 1)).start()
 
         return carry
 
@@ -264,17 +345,22 @@
         chunks = spins // ROWS
         by_pairs = n * (n + 1) // 2 <= window_start.shape[0]
         table = (n * n, LANES) if by_pairs else (n + 1, ROWS, width)
-        smem = pl.BlockSpec(memory_space=pltpu.SMEM)
         return pl.pallas_call(
             functools.partial(kernel, n, bands, by_pairs),
             out_shape=pltpu.VMEM((spins, width), jnp.float32),
-            in_specs=[pl.BlockSpec(memory_space=pl.ANY), smem, smem, smem],
+            in_specs=[pl.BlockSpec(memory_space=pl.ANY)] * 4,
             out_specs=pl.BlockSpec(memory_space=pltpu.VMEM),
             scratch_shapes=[
                 pltpu.VMEM((spins, bins + 2 * LANES), jnp.float32),
                 pltpu.VMEM((2, n, spins, width), jnp.float32),
                 pltpu.VMEM((spins, LANES), jnp.int32),
                 pltpu.VMEM(table, jnp.float32),
+                pltpu.SMEM(bin_shifts.shape, jnp.int32),
+                pltpu.SMEM(window_start.shape, jnp.int32),
+                pltpu.SMEM(window_length.shape, jnp.int32),
+                pltpu.SemaphoreType.REGULAR,
+                pltpu.SemaphoreType.REGULAR,
+                pltpu.SemaphoreType.DMA((3,)),
                 pltpu.SemaphoreType.DMA((chunks,)),
                 pltpu.SemaphoreType.DMA((chunks, n)),
                 pltpu.SemaphoreType.DMA((chunks, n)),

time: 54 us -> 53.1 us (0.983)
  Pallas kernels: 53.2 us -> 52.2 us
    pallas_call x1, Pallas kernels: 53.2 us -> 52.2 us  [on_device(): pl.pallas_call(functools.partial(kernel, n, bands, by_pairs), out_shape=p...]
where the time goes in v3:
time: 53.1 us; the launch traced here: 52.9 us
  Pallas kernels  52.2 us (98%)
  local copies, waits for them, and re-layouts  0.71 us (1%)
    pallas_call x1, Pallas kernels, on_device(): pl.pallas_call(functools.partial(kernel, n, bands, by_pairs), out_shape=p...  52.2 us

profile of v3, /device:TPU:9, one launch (start us, length us, event | category | flops | bytes accessed | tf_op | source)
XLA Modules:
  0.0 52.9 jit_solution(18225977880943035709)
XLA Ops:
  0.0 52.2 %shard_map.46 = f32[32,2048]{1,0:T(8,128)S(1)} custom-call(f32[1,32,16384]{2,1,0:T(8,128)} %maps.1, s32[1,32]{1,0:T(1,128)} %shifts_in.1, s32[256]{0:T(256)} %starts_in.1, s32[256]{0:T(256)} %lengths_in.1), custom_call_target="tpu_custom_call" | custom-call | tf_op jit(solution)/shard_map/pallas_call | solution.py:348
  52.2 0.7 %copy.6 = f32[32,2048]{1,0:T(8,128)} copy(f32[32,2048]{1,0:T(8,128)S(1)} %shard_map.46) | data formatting | bytes 524288

commit v4 on v3

--- a/solution.py
+++ b/solution.py
@@ -111,6 +111,38 @@
         for row in range(ROWS):
             amounts = jnp.where(sublane == row, shifts[0, chunk * ROWS + row], amounts)
         shift_rows[chunk * ROWS:(chunk + 1) * ROWS, :] = amounts
+
+    def partner(chunk, place):
+        later = order(me, place, n)
+        if not early:
+            return later
+        ends, mids = jnp.int32(0), jnp.int32(0)
+        for i, (end, mid) in enumerate(zip((2, 3, 1, 4, 5, 6, 7), (6, 7, 1, 2, 3, 4, 5))):
+            ends, mids = jnp.where(place == i, end, ends), jnp.where(place == i, mid, mids)
+        return jnp.where(chunk == 0, flipped(me, jnp.where(middle, mids, ends), n), later)
+
+    def align(chunk, dest, own):
+        rows = rows_of(chunk)
+        position = lane + shift_rows[rows, :]
+        index = position & (LANES - 1)
+        below, above = position < 0, position >= LANES
+
+        def turned(tile):
+            columns = pl.ds(pl.multiple_of(dest * width + tile * LANES, LANES), LANES)
+            return jnp.take_along_axis(wide[rows, columns], index, axis=1, mode="promise_in_bounds")
+
+        side = jnp.where(own, 1, 0)
+        before, here = turned(0), turned(1)
+        for tile in range(tiles):
+            after = turned(tile + 2)
+            blocks[side, dest, rows, tile * LANES:(tile + 1) * LANES] = jnp.where(
+                below, before, jnp.where(above, after, here)
+            )
+            before, here = here, after
+
+    if early:
+        loading(0).wait()
+        align(0, partner(0, 0), False)
 
     neighbours = jnp.where(band > 0, 1, 0) + jnp.where(band < bands - 1, 1, 0)
     pl.semaphore_wait(barrier, 3 + neighbours)
@@ -186,21 +218,12 @@
             device_id_type=MESH,
         )
 
-    def partner(chunk, place):
-        later = order(me, place, n)
-        if not early:
-            return later
-        ends, mids = jnp.int32(0), jnp.int32(0)
-        for i, (end, mid) in enumerate(zip((2, 3, 1, 4, 5, 6, 7), (6, 7, 1, 2, 3, 4, 5))):
-            ends, mids = jnp.where(place == i, end, ends), jnp.where(place == i, mid, mids)
-        return jnp.where(chunk == 0, flipped(me, jnp.where(middle, mids, ends), n), later)
-
     def step(i, carry):
         chunk, place = i // n, i % n
         own = place == n - 1
         dest = jnp.where(own, me, partner(chunk, place))
 
-        @pl.when(place == 0)
+        @pl.when((place == 0) & ((chunk > 0) | (not early)))
         def _():
             loading(chunk).wait()
 
@@ -212,23 +235,9 @@
         def _():
             halo(1, band + 1).wait_recv()
 
-        rows = rows_of(chunk)
-        position = lane + shift_rows[rows, :]
-        index = position & (LANES - 1)
-        below, above = position < 0, position >= LANES
-
-        def turned(tile):
-            columns = pl.ds(pl.multiple_of(dest * width + tile * LANES, LANES), LANES)
-            return jnp.take_along_axis(wide[rows, columns], index, axis=1, mode="promise_in_bounds")
-
-        side = jnp.where(own, 1, 0)
-        before, here = turned(0), turned(1)
-        for tile in range(tiles):
-            after = turned(tile + 2)
-            blocks[side, dest, rows, tile * LANES:(tile + 1) * LANES] = jnp.where(
-                below, before, jnp.where(above, after, here)
-            )
-            before, here = here, after
+        @pl.when(i > 0 if early else i >= 0)
+        def _():
+            align(chunk, dest, own)
 
         if early:
             @pl.when((chunk == 0) & (place == 4))
@@ -290,7 +299,7 @@
             out[rows, columns] = best
             return carry
 
-        lax.fori_loop(0, width // group, search, 0)
+        lax.fori_loop(0, width // group, search, 0, unroll=4 if width // group % 4 == 0 else 1)
 
     def search_windows(chunk):
         rows = rows_of(chunk)

time: 53.1 us -> 52.7 us (level)
  no operation moved by 1% of the time
where the time goes in v4:
time: 52.7 us; the launch traced here: 52.6 us
  Pallas kernels  51.9 us (98%)
  local copies, waits for them, and re-layouts  0.71 us (1%)
    pallas_call x1, Pallas kernels, on_device(): pl.pallas_call(functools.partial(kernel, n, bands, by_pairs), out_shape=p...  51.9 us

profile of v4, /device:TPU:9, one launch (start us, length us, event | category | flops | bytes accessed | tf_op | source)
XLA Modules:
  0.0 52.6 jit_solution(13918234071097624285)
XLA Ops:
  0.0 51.9 %shard_map.46 = f32[32,2048]{1,0:T(8,128)S(1)} custom-call(f32[1,32,16384]{2,1,0:T(8,128)} %maps.1, s32[1,32]{1,0:T(1,128)} %shifts_in.1, s32[256]{0:T(256)} %starts_in.1, s32[256]{0:T(256)} %lengths_in.1), custom_call_target="tpu_custom_call" | custom-call | tf_op jit(solution)/shard_map/pallas_call | solution.py:357
  51.9 0.7 %copy.6 = f32[32,2048]{1,0:T(8,128)} copy(f32[32,2048]{1,0:T(8,128)S(1)} %shard_map.46) | data formatting | bytes 524288
